TPU v7x, 256 devices: a 4x2x16 block of a 4x16x16 slice. The times are simulated.
256 devices in a mesh: groups: 2 (over y), space: 16 (over z), mp: 4 (over x), sub: 2 (over core).
Axes of the slice: x: 4, y: 2, z: 16, core: 2. Of those that a mesh axis runs over, the one named last changes fastest.
The devices are a block of a 4x16x16 slice.
Arguments:
- voxels: bfloat16 [98304, 512], P(('groups', 'space', 'sub')), parts along dimension 0, may hold values from -6 to 6
- window_ids: int32 [98304], P(('groups', 'space', 'sub')), parts along dimension 0, may hold values from 0 to 511, as said below
- voxel_slots: int32 [98304], P(('groups', 'space', 'sub')), parts along dimension 0, may hold values from 0 to 255, as said below
- window_counts: int32 [1024], P('groups'), parts along dimension 0, may hold values from 0 to 256, as said below
- norm_gain: float32 [512], replicated, may hold values from 0.25 to 1.75
- w_query_key: bfloat16 [2, 512, 512], P(None, None, 'mp'), may hold values from -2 to 2
- w_value: bfloat16 [512, 512], P(None, 'mp'), may hold values from -0.25 to 0.25
- w_out: bfloat16 [512, 512], P('mp'), may hold values from -0.25 to 0.25
- ffn_gain: float32 [512], replicated, may hold values from 0.25 to 1.75
- w_up: bfloat16 [512, 2048], P(None, 'mp'), may hold values from -0.25 to 0.25
- w_down: bfloat16 [2048, 512], P('mp'), may hold values from -0.125 to 0.125
Outputs:
- result: bfloat16 [98304, 512], P(('groups', 'space', 'sub'), 'mp'), parts along dimension 0
There are 2 independent parts, one for each index of `groups`. A program takes and returns all parts, laid end to end along the dimension named above; an argument that names none is the same for every part. Nothing has to cross between parts.
Inputs may be any that keep to these rules, and one draw needn't show every extreme that they name: `window_ids`: window w belongs to owner w // 16 (its index along space+sub) as that owner's window w % 16. On the voxels of one device at most 96 lie in windows of one owner, and in every draw some owner has exactly 96 voxels of every device. `voxel_slots`: the voxels of a window hold slots 0 to its count - 1, each once. window_counts[w] is the number of voxels with window id w; some window holds 256.
All inputs are finite; a program needn't handle non-finite values.
Results may differ from a plain program's by a relative error of at most 0.012.
Values may be sent and summed in bfloat16 or wider, within the bound.
A program may use at most 64 MiB of HBM per device.

v0:
```python
import jax
import jax.numpy as jnp
from jax import lax
from jax.sharding import PartitionSpec as P

HDIM = 64
WLEN = 256
WIN_DEV = 16


def in_blocks(value, dim, size):
    lengths = value.shape
    pieces = value.reshape(*lengths[:dim], size, lengths[dim] // size, *lengths[dim + 1 :])
    return jnp.moveaxis(pieces, dim, 0)


def in_order(pieces, dim):
    pieces = jnp.moveaxis(pieces, 0, dim)
    lengths = pieces.shape
    return pieces.reshape(*lengths[:dim], lengths[dim] * lengths[dim + 1], *lengths[dim + 2 :])


def joined_exchange(value, axis, axes, splits, concats):
    sizes = [lax.axis_size(a) for a in axes]
    pieces = in_blocks(value, splits[0], sizes[0])
    pieces = jnp.moveaxis(in_blocks(pieces, splits[1] + 1, sizes[1]), 0, 1)
    inside = pieces.shape[2:]
    pieces = pieces.reshape(-1, *inside)
    pieces = lax.all_to_all(pieces, axis, split_axis=0, concat_axis=0, tiled=True)
    pieces = in_order(pieces.reshape(*sizes, *inside), concats[0] + 1)
    return in_order(pieces, concats[1])


def rows_first(arrays, axis, dims):
    turned = [jnp.moveaxis(a, dim, 0) for a, dim in zip(arrays, dims)]
    widths = [t[0].size for t in turned]
    both = jnp.concatenate([t.reshape(-1, w) for t, w in zip(turned, widths)], axis=1)
    whole = lax.all_gather(both, axis, axis=0, tiled=True)
    pieces = jnp.split(whole, [sum(widths[:k]) for k in range(1, len(widths))], axis=1)
    return tuple(
        (
            jnp.moveaxis(b.reshape(-1, *t.shape[1:]), 0, dim)
            for b, t, dim in zip(pieces, turned, dims)
        )
    )


def summed_on_arrival(value, axis, dim):
    size = lax.axis_size(axis)
    pieces = lax.all_to_all(in_blocks(value, dim, size), axis, 0, 0, tiled=True)
    return jnp.sum(pieces.astype(jnp.float32), axis=0)


def normalize(values_in, gain):
    row_mean = jnp.mean(values_in, axis=-1, keepdims=True)
    centred = values_in - row_mean
    variance = jnp.mean(centred * centred, axis=-1, keepdims=True)
    return centred * lax.rsqrt(variance + 1e-05) * gain


def project(rows_in, weight):
    return jnp.dot(rows_in, weight, preferred_element_type=jnp.float32).astype(jnp.bfloat16)


def feed_forward(normed_in, up_proj, down_proj):
    hidden = jax.nn.gelu(
        jnp.dot(normed_in, up_proj, preferred_element_type=jnp.float32), approximate=True
    ).astype(jnp.bfloat16)
    return jnp.dot(hidden, down_proj, preferred_element_type=jnp.float32)


def regroup(send_rows, send_spots):
    space_size = lax.axis_size("space")
    sub_size = lax.axis_size("sub")
    rows_split = send_rows.reshape((space_size, sub_size) + send_rows.shape[1:])
    spots_split = send_spots.reshape((space_size, sub_size) + send_spots.shape[1:])
    received, received_spots = (
        joined_exchange(rows_split, ("space", "sub"), ("space", "sub"), (0, 1), (0, 1)),
        joined_exchange(spots_split, ("space", "sub"), ("space", "sub"), (0, 1), (0, 1)),
    )
    return (received.reshape(send_rows.shape), received_spots.reshape(send_spots.shape))


def send_back(send_rows):
    space_size = lax.axis_size("space")
    sub_size = lax.axis_size("sub")
    rows_split = send_rows.reshape((space_size, sub_size) + send_rows.shape[1:])
    received = lax.all_to_all(
        lax.all_to_all(rows_split, "sub", split_axis=1, concat_axis=1, tiled=True),
        "space",
        split_axis=0,
        concat_axis=0,
        tiled=True,
    )
    return received.reshape(send_rows.shape)


def attend(queries, key_rows, values, counts):
    windows = counts.shape[0]
    window_len = queries.shape[0] // windows
    head_count = queries.shape[1] // HDIM
    split_shape = (windows, window_len, head_count, HDIM)
    scores = jnp.einsum(
        "wqhd,wkhd->whqk",
        queries.reshape(split_shape),
        key_rows.reshape(split_shape),
        preferred_element_type=jnp.float32,
    ) * HDIM ** (-0.5)
    live_keys = (jnp.arange(window_len, dtype=jnp.int32)[None, :] < counts[:, None])[
        :, None, None, :
    ]
    scores = jnp.where(live_keys, scores, jnp.float32(-1e30))
    row_max = jnp.max(scores, axis=-1, keepdims=True)
    weights = jnp.exp(scores - row_max)
    probabilities = (weights / jnp.sum(weights, axis=-1, keepdims=True)).astype(jnp.bfloat16)
    mixture = jnp.einsum(
        "whqk,wkhd->wqhd",
        probabilities,
        values.reshape(split_shape),
        preferred_element_type=jnp.float32,
    )
    return mixture.astype(jnp.bfloat16).reshape(windows * window_len, head_count * HDIM)


def shards(
    voxels,
    window_ids,
    voxel_slots,
    window_counts,
    norm_gain,
    w_query_key,
    w_value,
    w_out,
    ffn_gain,
    w_up,
    w_down,
):
    owner_total = lax.axis_size(("space", "sub"))
    my_index = lax.axis_index(("space", "sub"))
    row_count = voxels.shape[0]
    capacity = 2 * row_count // owner_total
    local_width = w_value.shape[1]
    stream = voxels.astype(jnp.float32)
    normed = normalize(stream, norm_gain).astype(jnp.bfloat16)
    destination = window_ids // WIN_DEV
    position = window_ids % WIN_DEV * WLEN + voxel_slots
    target = (destination[:, None] == jnp.arange(owner_total, dtype=jnp.int32)[None, :]).astype(
        jnp.int32
    )
    before = jnp.sum((jnp.cumsum(target, axis=0) - target) * target, axis=1)
    send_index = destination * capacity + before
    payload = jnp.concatenate(
        [
            project(normed, w_query_key[0]),
            project(normed, w_query_key[1]),
            project(normed, w_value),
        ],
        axis=1,
    )
    row_width = payload.shape[1]
    outgoing = (
        jnp.zeros((owner_total * capacity, row_width), jnp.bfloat16).at[send_index].set(payload)
    )
    out_spots = (
        jnp.full((owner_total * capacity,), WIN_DEV * WLEN, jnp.int32).at[send_index].set(position)
    )
    arrived, arrived_spots = regroup(
        outgoing.reshape(owner_total, capacity, row_width), out_spots.reshape(owner_total, capacity)
    )
    arrived = arrived.reshape(owner_total * capacity, row_width)
    arrived_spots = arrived_spots.reshape(owner_total * capacity)
    padded = (
        jnp.zeros((WIN_DEV * WLEN, row_width), jnp.bfloat16)
        .at[arrived_spots]
        .set(arrived, mode="drop")
    )
    queries = padded[:, :local_width]
    key_rows = padded[:, local_width : 2 * local_width]
    values = padded[:, 2 * local_width :]
    counts = lax.dynamic_slice_in_dim(window_counts, my_index * WIN_DEV, WIN_DEV, 0)
    mixture = attend(queries, key_rows, values, counts)
    answer = jnp.take(mixture, arrived_spots, axis=0, mode="clip").reshape(
        owner_total, capacity, local_width
    )
    answer = send_back(answer)
    attended = answer.reshape(owner_total * capacity, local_width)[send_index]
    head_rows = w_out.shape[0]
    all_heads, whole_out = rows_first((attended, w_out), "mp", (1, 0))
    after_attn = stream + jnp.dot(all_heads, whole_out, preferred_element_type=jnp.float32)
    ffn_terms = feed_forward(normalize(after_attn, ffn_gain).astype(jnp.bfloat16), w_up, w_down)
    remainder = lax.dynamic_slice_in_dim(after_attn, lax.axis_index("mp") * head_rows, head_rows, 1)
    result = summed_on_arrival(ffn_terms.astype(jnp.bfloat16), "mp", 1) + remainder
    return result.astype(jnp.bfloat16)


def solution(mesh):
    return jax.shard_map(
        shards,
        mesh=mesh,
        in_specs=(
            P(("groups", "space", "sub"), None),
            P(("groups", "space", "sub")),
            P(("groups", "space", "sub")),
            P("groups"),
            P(),
            P(None, None, "mp"),
            P(None, "mp"),
            P("mp", None),
            P(),
            P(None, "mp"),
            P("mp", None),
        ),
        out_specs=P(("groups", "space", "sub"), "mp"),
        check_vma=False,
    )
```

profile of v0, /device:TPU:168, one launch (start us, length us, event | category | flops | bytes accessed | tf_op | source)
XLA Modules:
  0.0 378.7 jit_solution(3813832232292492502)
XLA Ops:
  7.4 9.1 %reduce-window.6 = s32[32,12,128]{2,1,0:T(8,128)S(1)} reduce-window(s32[32,12,128]{2,1,0:T(8,128)S(1)} %fusion.39, s32[]{:T(128)} %constant.33.clone.1), window={size=1x1x128 pad=0_0x0_0x127_0}, to_apply=%region_0.0 | reduce-window | flops 6242304 | bytes 393220 | tf_op jit(solution)/shard_map/reduce-window
  17.1 6.2 %scatter_custom_fusion = s32[3072]{0:T(1024)S(1)} fusion(s32[1536]{0:T(1024)S(1)} %compare_select_fusion.1, s32[1536]{0:T(1024)S(1)} %get-tuple-element.8, s32[]{:T(128)} %constant.29.clone.1), kind=kCustom, calls=%fused_computation.85 | custom fusion | bytes 12292 | tf_op jit(solution)/shard_map/scatter | solution.py:165
  24.0 23.3 %all-to-all-start = ((s32[32,1,1,96]{3,2,1,0:T(1,128)}), s32[32,1,1,96]{3,2,1,0:T(1,128)S(1)}, u32[]{:S(2)}, u32[]{:S(2)}) async-start(s32[32,1,1,96]{3,2,1,0:T(1,128)} %reshape_transpose_transpose_reshape_reshape_reshape_reshape.6), calls=%async_computation | async-start | bytes 32768 | tf_op jit(solution)/shard_map/all_to_all | solution.py:29
  53.5 9.4 %scatter_custom_fusion.1 = bf16[3072,384]{1,0:T(8,128)(2,1)} fusion(s32[1536]{0:T(1024)S(1)} %compare_select_fusion.1, bf16[1536,384]{1,0:T(8,128)(2,1)} %copy.65, bf16[]{:T(256)} %constant.28.clone.1), kind=kCustom, calls=%fused_computation.52 | custom fusion | bytes 2359808 | tf_op jit(solution)/shard_map/scatter | solution.py:162
  62.9 12.4 %all-to-all-start.1 = ((bf16[32,1,1,96,384]{4,3,2,1,0:T(8,128)(2,1)}), bf16[32,1,1,96,384]{4,3,2,1,0:T(8,128)(2,1)}, u32[]{:S(2)}, u32[]{:S(2)}) async-start(bf16[32,1,1,96,384]{4,3,2,1,0:T(8,128)(2,1)} %bitcast.62), calls=%async_computation.1 | async-start | bytes 4718592 | tf_op jit(solution)/shard_map/all_to_all | solution.py:29
  76.4 110.3 %all-to-all-done.1 = bf16[32,1,1,96,384]{4,3,2,1,0:T(8,128)(2,1)} async-done(((bf16[32,1,1,96,384]{4,3,2,1,0:T(8,128)(2,1)}), bf16[32,1,1,96,384]{4,3,2,1,0:T(8,128)(2,1)}, u32[]{:S(2)}, u32[]{:S(2)}) %all-to-all-start.1) | async-done | bytes 2359328 | tf_op jit(solution)/shard_map/all_to_all | solution.py:29
  186.7 16.2 %scatter_custom_fusion.2 = bf16[4096,384]{1,0:T(8,128)(2,1)} fusion(s32[3072]{0:T(1024)S(1)} %bitcast.72, bf16[3072,384]{1,0:T(8,128)(2,1)} %bitcast.16, bf16[]{:T(256)} %constant.28.clone.1), kind=kCustom, calls=%fused_computation.47 | custom fusion | bytes 3146240 | tf_op jit(solution)/shard_map/scatter | solution.py:175
  202.9 3.4 fusion.62
  206.3 5.0 %reshape.172 = bf16[16,256,2,64]{3,2,1,0:T(2,128)(2,1)} reshape(bf16[4096,128]{1,0:T(8,128)(2,1)} %get-tuple-element.7) | data formatting | bytes 2097152 | tf_op jit(solution)/shard_map/reshape | solution.py:105
  211.3 5.0 %reshape.173 = bf16[16,256,2,64]{3,2,1,0:T(2,128)(2,1)} reshape(bf16[4096,128]{1,0:T(8,128)(2,1)} %get-tuple-element.6) | data formatting | bytes 2097152 | tf_op jit(solution)/shard_map/reshape | solution.py:106
  218.2 3.5 fusion.19
  221.7 4.2 %fusion.63 = (f32[16,2,256]{2,1,0:T(2,128)S(1)}, f32[16,2,256,256]{2,3,1,0:T(8,128)S(1)}) fusion(f32[16,2,256,256]{2,3,1,0:T(8,128)S(1)} %fusion.19, pred[16,256]{1,0:T(8,128)(4,1)S(1)} %iota_compare_fusion.2), kind=kOutput, calls=%fused_computation.97 | output fusion | flops 12583167 | bytes 16814080 | tf_op jit(solution)/shard_map/sub | solution.py:114
  226.9 3.8 copy.87
  230.6 3.9 %reshape.174 = bf16[4096,128]{1,0:T(8,128)(2,1)S(1)} reshape(bf16[16,256,2,64]{3,2,1,0:T(2,128)(2,1)} %copy.87) | data formatting | bytes 2097152 | tf_op jit(solution)/shard_map/reshape | solution.py:122
  234.5 11.4 %gather_fusion = bf16[3072,128]{1,0:T(8,128)(2,1)} fusion(bf16[4096,128]{1,0:T(8,128)(2,1)S(1)} %reshape.174, s32[3072]{0:T(1024)S(1)} %broadcast_clamp_fusion), kind=kCustom, calls=%fused_computation | custom fusion | bytes 1585152 | tf_op jit(solution)/shard_map/jit(_take)/gather | solution.py:182
  247.2 4.4 %all_to_all.25 = bf16[16,2,96,128]{3,2,0,1:T(8,128)(2,1)S(1)} all-to-all(bf16[16,2,96,128]{3,2,0,1:T(8,128)(2,1)S(1)} %copy.76), channel_id=1, replica_groups=mesh['groups'=2,'space'=16,'mp'=4,'sub'=2] {'sub'}, dimensions={1} | all-to-all | bytes 1572864 | tf_op jit(solution)/shard_map/all_to_all | solution.py:89
  252.5 3.8 all-to-all-start.3
  256.7 39.0 %all-to-all-done.3 = bf16[16,2,96,128]{3,2,1,0:T(8,128)(2,1)S(1)} async-done(((bf16[16,2,96,128]{3,2,1,0:T(8,128)(2,1)}), bf16[16,2,96,128]{3,2,1,0:T(8,128)(2,1)S(1)}, u32[]{:S(2)}, u32[]{:S(2)}) %all-to-all-start.3) | async-done | bytes 786464 | tf_op jit(solution)/shard_map/all_to_all | solution.py:88
  295.8 3.2 gather_fusion.1
  299.9 36.2 %all-gather.2.cloned.1.call-done = bf16[512,2048]{0,1:T(8,128)(2,1)} async-done(((bf16[128,2048]{0,1:T(8,128)(2,1)}), bf16[512,2048]{0,1:T(8,128)(2,1)}) %all-gather.2.cloned.1.call-update) | async-done | bytes 2097168 | tf_op jit(solution)/shard_map/all_gather | solution.py:38
  336.1 2.5 fusion.64
  340.8 5.4 %convolution_convert_fusion = bf16[1536,512]{0,1:T(8,128)(2,1)} fusion(bf16[512,512]{1,0:T(8,128)(2,1)S(1)} %copy-done, bf16[512,512]{1,0:T(8,128)(2,1)S(1)} %copy-done.4, f32[1536,512]{0,1:T(8,128)} %copy-done.1, f32[512]{0:T(512)S(1)} %copy-done.8, f32[1536]{0:T(1024)S(1)} %add_rsqrt_fusion, f32[1536]{0:T(1024)S(1)} %broadcast_multiply_fusion), kind=kOutput, calls=%fused_computation.34 | convolution fusion | flops 1621622784 | bytes 5781504 | tf_op jit(solution)/shard_map/dot_general | solution.py:69
  346.1 4.0 %all-to-all-start.4 = ((bf16[4,1536,128]{1,2,0:T(8,128)(2,1)}), bf16[4,1536,128]{1,2,0:T(8,128)(2,1)S(1)}, u32[]{:S(2)}, u32[]{:S(2)}) async-start(bf16[4,1536,128]{1,2,0:T(8,128)(2,1)} %bitcast.64), calls=%async_computation.4 | async-start | bytes 3145728 | tf_op jit(solution)/shard_map/all_to_all | solution.py:50
  350.1 19.3 %all-to-all-done.4 = bf16[4,1536,128]{1,2,0:T(8,128)(2,1)S(1)} async-done(((bf16[4,1536,128]{1,2,0:T(8,128)(2,1)}), bf16[4,1536,128]{1,2,0:T(8,128)(2,1)S(1)}, u32[]{:S(2)}, u32[]{:S(2)}) %all-to-all-start.4) | async-done | bytes 1572896 | tf_op jit(solution)/shard_map/all_to_all | solution.py:50
  (60 shorter events, 20.1 us)
Async XLA Ops:
  6.5 334.2 %copy-start = (bf16[512,512]{1,0:T(8,128)(2,1)S(1)}, bf16[512,512]{1,0:T(8,128)(2,1)}, u32[]{:S(2)}) copy-start(bf16[512,512]{1,0:T(8,128)(2,1)} %param.21) | copy-start | bytes 1572868
  24.0 38.9 %all-to-all-start = ((s32[32,1,1,96]{3,2,1,0:T(1,128)}), s32[32,1,1,96]{3,2,1,0:T(1,128)S(1)}, u32[]{:S(2)}, u32[]{:S(2)}) async-start(s32[32,1,1,96]{3,2,1,0:T(1,128)} %reshape_transpose_transpose_reshape_reshape_reshape_reshape.6), calls=%async_computation | async-start | bytes 32768 | tf_op jit(solution)/shard_map/all_to_all | solution.py:29
  47.3 2.5 copy-start.5
  47.3 2.5 copy-start.7
  49.9 1.4 copy-start.6
  62.9 123.8 %all-to-all-start.1 = ((bf16[32,1,1,96,384]{4,3,2,1,0:T(8,128)(2,1)}), bf16[32,1,1,96,384]{4,3,2,1,0:T(8,128)(2,1)}, u32[]{:S(2)}, u32[]{:S(2)}) async-start(bf16[32,1,1,96,384]{4,3,2,1,0:T(8,128)(2,1)} %bitcast.62), calls=%async_computation.1 | async-start | bytes 4718592 | tf_op jit(solution)/shard_map/all_to_all | solution.py:29
  221.7 4.2 %copy-start.2 = (bf16[16,256,2,64]{3,2,1,0:T(2,128)(2,1)S(1)}, bf16[16,256,2,64]{3,2,1,0:T(2,128)(2,1)}, u32[]{:S(2)}) copy-start(bf16[16,256,2,64]{3,2,1,0:T(2,128)(2,1)} %reshape.171) | copy-start | bytes 3145732
  246.0 10.6 %copy-start.3 = (bf16[128,512]{1,0:T(8,128)(2,1)S(1)}, bf16[128,512]{1,0:T(8,128)(2,1)}, u32[]{:S(2)}) copy-start(bf16[128,512]{1,0:T(8,128)(2,1)} %param.18) | copy-start | bytes 393220
  252.5 43.3 %all-to-all-start.3 = ((bf16[16,2,96,128]{3,2,1,0:T(8,128)(2,1)}), bf16[16,2,96,128]{3,2,1,0:T(8,128)(2,1)S(1)}, u32[]{:S(2)}, u32[]{:S(2)}) async-start(bf16[16,2,96,128]{3,2,1,0:T(8,128)(2,1)} %copy.77), calls=%async_computation.3 | async-start | bytes 1572864 | tf_op jit(solution)/shard_map/all_to_all | solution.py:88
  256.3 79.8 %all-gather.2.cloned.1.call-start = ((), (), s32[]{:S(2)}) async-start(), calls=%async_computation.5 | async-start | bytes 2621440 | tf_op jit(solution)/shard_map/all_gather | solution.py:38
  338.7 1.7 copy-start.1
  338.7 2.1 copy-start.4
  338.7 2.1 copy-start.8
  346.1 23.3 %all-to-all-start.4 = ((bf16[4,1536,128]{1,2,0:T(8,128)(2,1)}), bf16[4,1536,128]{1,2,0:T(8,128)(2,1)S(1)}, u32[]{:S(2)}, u32[]{:S(2)}) async-start(bf16[4,1536,128]{1,2,0:T(8,128)(2,1)} %bitcast.64), calls=%async_computation.4 | async-start | bytes 3145728 | tf_op jit(solution)/shard_map/all_to_all | solution.py:50
Sparse Core Ops, SparseCore 0:
  300.0 36.0 all-gather.1
where the time goes:
time: 381 us; the launch traced here: 379 us
  waiting for transfers between devices  205 us (54%)
  local copies, waits for them, and re-layouts  79.4 us (21%)
  starting transfers between devices  43.8 us (11%)
  other arithmetic  18 us (5%)
  matrix products  14.5 us (4%)
  between operations  13.8 us (4%)
  blocking collectives  4.38 us (1%)
    all_to_all x2, waiting for transfers between devices, joined_exchange(): lax.all_to_all(pieces, axis, split_axis=0, concat_axis=0, tiled=True)  110 us
    all_to_all x1, waiting for transfers between devices, send_back(): lax.all_to_all(lax.all_to_all(rows_split, 'sub', split_axis=1, concat_axi...  39 us
    all_gather x1, waiting for transfers between devices, rows_first(): whole = lax.all_gather(both, axis, axis=0, tiled=True)  36.2 us
    all_to_all x2, starting transfers between devices, joined_exchange(): lax.all_to_all(pieces, axis, split_axis=0, concat_axis=0, tiled=True)  35.7 us
    all_to_all x1, waiting for transfers between devices, summed_on_arrival(): pieces = lax.all_to_all(in_blocks(value, dim, size), axis, 0, 0, tiled=True)  19.3 us
    scatter x1, local copies, waits for them, and re-layouts, shards(): padded = jnp.zeros((WIN_DEV * WLEN, row_width), jnp.bfloat16).at[arrived_...  16.2 us
    gather x1, local copies, waits for them, and re-layouts, shards(): jnp.take(mixture, arrived_spots, axis=0, mode='clip')  11.4 us
    scatter x1, local copies, waits for them, and re-layouts, shards(): jnp.zeros((owner_total * capacity, row_width), jnp.bfloat16).at[send_index]  9.38 us
  transfers between devices with their start and end apart: 5, of which 4 were waited for; matrix products, arithmetic and copies ran while one was open for 4% of the time, Pallas kernels for 0%

commit v1 on v0

v1 whole, which is shorter than its diff:
```python
import functools

import jax
import jax.numpy as jnp
from jax import lax
from jax.experimental import pallas as pl
from jax.experimental.pallas import tpu as pltpu
from jax.sharding import PartitionSpec as P

HDIM = 64
WLEN = 256
WIN_DEV = 16
LANES = 128
MESH = pl.DeviceIdType.MESH
BF16 = jnp.bfloat16
F32 = jnp.float32


def dot(a, b):
    return jnp.dot(a, b, preferred_element_type=F32)


def dot_nt(a, b):
    return lax.dot_general(a, b, (((1,), (1,)), ((), ())), preferred_element_type=F32)


def dot_tn(a, b):
    return lax.dot_general(a, b, (((0,), (0,)), ((), ())), preferred_element_type=F32)


def pick(mask):
    return jnp.where(mask, 1.0, 0.0).astype(BF16)


def block_kernel(
    sizes,
    x_ref,
    ids_ref,
    slots_ref,
    counts_ref,
    gain_ref,
    wqk_ref,
    wv_ref,
    wo_ref,
    fgain_ref,
    wu_ref,
    wd_ref,
    out_ref,
    xn,
    packed,
    spot_out,
    spot_in,
    arr,
    spot_col,
    send_col,
    acc,
    mixt,
    ans,
    ret,
    att,
    attx,
    res,
    resx,
    wo_all,
    wu_all,
    wd_all,
    z_send,
    z_recv,
    s_send,
    s_recv,
    x_send,
    x_recv,
    b_send,
    b_recv,
    w_send,
    w_recv,
    d_send,
    d_recv,
    a_send,
    a_recv,
    r_send,
    r_recv,
):
    nz, nm, ns = sizes
    rows, width = x_ref.shape
    owners = nz * ns
    cap = 2 * rows // owners
    groups = nz // 2
    per = 2 * ns
    grows = per * cap
    quarter = rows // nm
    z = lax.axis_index("space")
    m = lax.axis_index("mp")
    s = lax.axis_index("sub")
    me = z * ns + s
    mcols = pl.ds(pl.multiple_of(m * LANES, LANES), LANES)

    def offset(g, j):
        if g == 0:
            return (0 if j < ns else nz // 2), j % ns
        return (g if j < ns else nz - g), j % ns

    def forward(g, j):
        dz, ds = offset(g, j)
        return lax.rem(z + dz, nz), lax.rem(s + ds, ns)

    def backward(g, j):
        dz, ds = offset(g, j)
        return lax.rem(z + (nz - dz), nz), lax.rem(s + ds, ns)

    def owner(g, j):
        tz, ts = forward(g, j)
        return tz * ns + ts

    def first(g):
        return 1 if g == 0 else 0

    def remote(src, dst, ssem, rsem, **where):
        return pltpu.make_async_remote_copy(
            src_ref=src,
            dst_ref=dst,
            send_sem=ssem,
            recv_sem=rsem,
            device_id=where,
            device_id_type=MESH,
        )

    order = [0] + list(range(groups - 1, 0, -1))
    others = [lax.rem(m + k, nm) for k in range(1, nm)]

    barrier = pltpu.get_barrier_semaphore()
    for g in range(groups):
        for j in range(first(g), per):
            tz, ts = forward(g, j)
            pl.semaphore_signal(
                barrier, inc=1, device_id={"space": tz, "sub": ts}, device_id_type=MESH
            )
    for om in others:
        pl.semaphore_signal(barrier, inc=1, device_id={"mp": om}, device_id_type=MESH)

    def norm_rows(i, carry):
        at = pl.ds(pl.multiple_of(i * 256, 256), 256)
        xb = x_ref[at, :].astype(F32)
        mean = jnp.sum(xb, axis=1, keepdims=True) * (1.0 / width)
        cen = xb - mean
        var = jnp.sum(cen * cen, axis=1, keepdims=True) * (1.0 / width)
        mine = x_ref[at, mcols].astype(F32) - mean
        xn[at, :] = (mine * lax.rsqrt(var + 1e-05) * gain_ref[:, mcols]).astype(BF16)
        return carry

    lax.fori_loop(0, rows // 256, norm_rows, 0)

    ids = ids_ref[...]
    dest = ids // WIN_DEV
    win = ids - dest * WIN_DEV
    owner_iota = lax.broadcasted_iota(jnp.int32, (owners, rows), 0)
    hit = owner_iota == dest
    table = pick(hit)
    step = 256
    earlier = pick(
        lax.broadcasted_iota(jnp.int32, (step, step), 0)
        < lax.broadcasted_iota(jnp.int32, (step, step), 1)
    )
    seen = jnp.zeros((owners, 1), F32)
    ranks = []
    for i in range(rows // step):
        part = table[:, i * step : (i + 1) * step]
        wide = part.astype(F32)
        before = dot(part, earlier) + seen
        ranks.append(jnp.sum(before * wide, axis=0, keepdims=True))
        seen = seen + jnp.sum(wide, axis=1, keepdims=True)
    rank = jnp.concatenate(ranks, axis=1).astype(jnp.int32)
    send = dest * cap + rank
    rank_hit = pick(lax.broadcasted_iota(jnp.int32, (LANES, rows), 0) == rank)
    slot_at = dot_nt(
        jnp.where(hit, (slots_ref[...] + 1).astype(F32), 0.0).astype(BF16), rank_hit
    )
    win_at = dot_nt(jnp.where(hit, win.astype(F32), 0.0).astype(BF16), rank_hit)
    spots = slot_at + win_at * float(WLEN)
    for o in range(owners):
        spot_out[o] = spots[o : o + 1, :]

    pl.semaphore_wait(barrier, groups * per - 1 + nm - 1)

    row_in = lax.broadcasted_iota(jnp.int32, (grows, 1), 0)
    lane_in = lax.broadcasted_iota(jnp.int32, (1, grows), 1)

    def places(g, inner):
        total = inner
        for j in range(per):
            low = owner(g, j) * cap - j * cap
            if j == 0:
                total = inner + low
            else:
                total = jnp.where(inner >= j * cap, inner + low, total)
        return total

    xn_all = xn[...]
    for g in order:
        for j in range(first(g), per):
            tz, ts = forward(g, j)
            remote(
                spot_out.at[owner(g, j)],
                spot_in.at[g, j],
                s_send.at[g],
                s_recv.at[g],
                space=tz,
                sub=ts,
            ).start()
        sel = pick(places(g, row_in) == send)
        packed[g] = dot(sel, xn_all).astype(BF16).reshape(per, cap, LANES)
        for j in range(first(g), per):
            tz, ts = forward(g, j)
            remote(
                packed.at[g, j],
                arr.at[g, j, :, mcols],
                z_send.at[g],
                z_recv.at[g],
                space=tz,
                sub=ts,
            ).start()

    arr[0, 0, :, mcols] = packed[0, 0]
    spot_in[0, 0] = spot_out[me]
    wo_all[m] = wo_ref[...]
    wu_all[m] = wu_ref[...]
    wd_all[m] = wd_ref[...]
    for i in range(rows // LANES):
        piece = send[:, i * LANES : (i + 1) * LANES].astype(F32)
        send_col[i * LANES : (i + 1) * LANES, :] = jnp.transpose(
            jnp.broadcast_to(piece, (LANES, LANES))
        )

    lane = lax.broadcasted_iota(jnp.int32, (1, LANES), 1)
    wqkv = jnp.concatenate([wqk_ref[0], wqk_ref[1], wv_ref[...]], axis=1)

    def spot_row(g):
        a0, a1, a2, a3 = (spot_in[g, j] for j in range(per))
        r1 = pltpu.roll(a1, 96, 1)
        r2 = pltpu.roll(a2, 64, 1)
        r3 = pltpu.roll(a3, 32, 1)
        t0 = a0 + jnp.where(lane >= 96, r1, 0.0)
        t1 = jnp.where(lane < 64, r1, 0.0) + jnp.where(lane >= 64, r2, 0.0)
        t2 = jnp.where(lane < 32, r2, 0.0) + jnp.where(lane >= 32, r3, 0.0)
        return [t0, t1, t2]

    def gather_wait(g):
        lo = first(g)
        remote(
            spot_out.at[pl.ds(0, per - lo)],
            spot_in.at[g, pl.ds(lo, per - lo)],
            s_send.at[g],
            s_recv.at[g],
            mp=others[0],
        ).wait_recv()
        remote(
            packed.at[g, pl.ds(lo, per - lo)],
            arr.at[g, pl.ds(lo, per - lo), :, mcols],
            z_send.at[g],
            z_recv.at[g],
            mp=others[0],
        ).wait_recv()

    def share(g, k):
        return remote(
            arr.at[g, :, :, mcols],
            arr.at[g, :, :, mcols],
            x_send.at[g, k],
            x_recv.at[g, k],
            mp=others[k],
        )

    def shared_wait(g):
        for k in range(nm - 1):
            share(g, k).wait_recv()

    def regroup(pair, fresh):
        parts = []
        for g in pair:
            tiles = spot_row(g)
            parts += tiles
            for i, t in enumerate(tiles):
                spot_col[g, i * LANES : (i + 1) * LANES, :] = jnp.transpose(
                    jnp.broadcast_to(t, (LANES, LANES))
                )
        row = jnp.concatenate(parts, axis=1).astype(jnp.int32)
        held = jnp.concatenate([arr[g].reshape(grows, width) for g in pair], axis=0)
        proj = dot(held, wqkv).astype(BF16)
        slot_iota = lax.broadcasted_iota(jnp.int32, (WLEN, row.shape[1]), 0) + 1

        def one_window(w, carry):
            got = dot(pick(slot_iota == row - w * WLEN), proj).astype(BF16)
            if fresh:
                acc[w] = got
            else:
                acc[w] = acc[w] + got
            return carry

        lax.fori_loop(0, WIN_DEV, one_window, 0)

    pairs = [order[i : i + 2] for i in range(0, groups, 2)]
    for i, pair in enumerate(pairs):
        for g in pair:
            gather_wait(g)
            for k in range(nm - 1):
                share(g, k).start()
        if i > 0:
            for g in pairs[i - 1]:
                shared_wait(g)
            regroup(pairs[i - 1], i == 1)

    def weight_parts(ref, all_ref, who):
        half = ref.shape[0] // ns
        at = pl.ds(pl.multiple_of(s * half, half), half)
        return ref.at[at], all_ref.at[who, at]

    def weight_copy(i, k):
        ref, all_ref = ((wu_ref, wu_all), (wd_ref, wd_all), (wo_ref, wo_all))[i]
        src, dst = weight_parts(ref, all_ref, m)
        return remote(src, dst, w_send.at[i, k], w_recv.at[i, k], mp=others[k])

    def weight_pass(i, k):
        ref, all_ref = ((wu_ref, wu_all), (wd_ref, wd_all), (wo_ref, wo_all))[i]
        src, dst = weight_parts(ref, all_ref, lax.rem(m + nm - 1 - k, nm))
        return remote(dst, dst, d_send.at[i, k], d_recv.at[i, k], sub=lax.rem(s + 1, ns))

    for i in range(3):
        for k in range(nm - 1):
            weight_copy(i, k).start()

    for g in pairs[-1]:
        shared_wait(g)
    regroup(pairs[-1], False)

    key_iota = lax.broadcasted_iota(jnp.int32, (WLEN, WLEN), 0)
    head_of = lax.broadcasted_iota(jnp.int32, (1, LANES), 1) // HDIM

    def attend(w, carry):
        here = acc[w]
        q = here[:, :LANES]
        k = here[:, LANES : 2 * LANES]
        v = here[:, 2 * LANES :]
        live = key_iota < counts_ref[me * WIN_DEV + w]
        parts = []
        vt = jnp.transpose(v.astype(F32)).astype(BF16)
        for h in range(LANES // HDIM):
            qh = jnp.where(head_of == h, q.astype(F32) * HDIM**-0.5, 0.0).astype(BF16)
            sc = jnp.where(live, dot_nt(k, qh), -1e30)
            weights = jnp.exp(sc - jnp.max(sc, axis=0, keepdims=True))
            total = jnp.sum(weights, axis=0, keepdims=True)
            mix = dot(vt[h * HDIM : (h + 1) * HDIM], weights.astype(BF16))
            parts.append(mix / total)
        at = pl.ds(pl.multiple_of(w * WLEN, WLEN), WLEN)
        mixt[:, at] = jnp.concatenate(parts, axis=0).astype(BF16)
        return carry

    lax.fori_loop(0, WIN_DEV, attend, 0)

    span = 4 * WLEN
    span_iota = lax.broadcasted_iota(jnp.int32, (1, span), 1)
    for g in order:
        col = spot_col[g].astype(jnp.int32)
        wide = jnp.concatenate([col] * (span // LANES), axis=1)

        def gather(c, total):
            at = pl.ds(pl.multiple_of(c * span, span), span)
            return total + dot_nt(pick(wide == span_iota + (c * span + 1)), mixt[:, at])

        total = lax.fori_loop(
            0, WIN_DEV * WLEN // span, gather, jnp.zeros((grows, LANES), F32)
        )
        ans[g] = total.astype(BF16).reshape(per, cap, LANES)
        for j in range(first(g), per):
            tz, ts = backward(g, j)
            remote(
                ans.at[g, j], ret.at[g, j], b_send.at[g], b_recv.at[g], space=tz, sub=ts
            ).start()
    ret[0, 0] = ans[0, 0]

    for i in range(3):
        for k in range(nm - 1):
            weight_copy(i, k).wait_recv()
            weight_pass(i, k).start()

    wide_send = send_col[...].astype(jnp.int32)
    wide_send = jnp.concatenate([wide_send] * (grows // LANES), axis=1)
    for n, g in enumerate(order):
        lo = first(g)
        remote(
            ans.at[g, pl.ds(lo, per - lo)],
            ret.at[g, pl.ds(lo, per - lo)],
            b_send.at[g],
            b_recv.at[g],
            mp=others[0],
        ).wait_recv()
        got = dot(
            pick(wide_send == places(g, lane_in)), ret[g].reshape(grows, LANES)
        ).astype(BF16)
        got = got.reshape(nm, quarter, LANES)
        if n == 0:
            att[...] = got
        else:
            att[...] = att[...] + got

    def head_copy(k):
        return remote(
            att.at[others[k]], attx.at[m], a_send.at[k], a_recv.at[k], mp=others[k]
        )

    for k in range(nm - 1):
        head_copy(k).start()
    attx[m] = att[m]
    for i in range(3):
        for k in range(nm - 1):
            weight_pass(i, k).wait_recv()
    for k in range(nm - 1):
        head_copy(k).wait_recv()

    heads = jnp.concatenate([attx[k] for k in range(nm)], axis=1)
    mine = pl.ds(pl.multiple_of(m * quarter, quarter), quarter)
    after = x_ref[mine, :].astype(F32) + dot(heads, wo_all[...].reshape(width, width))
    mean = jnp.sum(after, axis=1, keepdims=True) * (1.0 / width)
    cen = after - mean
    var = jnp.sum(cen * cen, axis=1, keepdims=True) * (1.0 / width)
    normed = (cen * lax.rsqrt(var + 1e-05) * fgain_ref[...]).astype(BF16)
    total = after
    for c in range(nm):
        up = dot(normed, wu_all[c])
        inner = 0.7978845608028654 * (up + 0.044715 * (up * up * up))
        hidden = (0.5 * up * (1.0 + jnp.tanh(inner))).astype(BF16)
        total = total + dot(hidden, wd_all[c])
    total = total.astype(BF16)
    for k in range(nm):
        res[k] = total[:, k * LANES : (k + 1) * LANES]

    def result_copy(k):
        return remote(
            res.at[others[k]], resx.at[m], r_send.at[k], r_recv.at[k], mp=others[k]
        )

    for k in range(nm - 1):
        result_copy(k).start()
    resx[m] = res[m]

    for g in range(groups):
        lo = first(g)
        at = pl.ds(lo, per - lo)
        remote(
            spot_out.at[pl.ds(0, per - lo)],
            spot_in.at[g, at],
            s_send.at[g],
            s_recv.at[g],
            mp=others[0],
        ).wait_send()
        remote(
            packed.at[g, at], arr.at[g, at, :, mcols], z_send.at[g], z_recv.at[g], mp=others[0]
        ).wait_send()
        remote(ans.at[g, at], ret.at[g, at], b_send.at[g], b_recv.at[g], mp=others[0]).wait_send()
        for k in range(nm - 1):
            share(g, k).wait_send()
    for k in range(nm - 1):
        for i in range(3):
            weight_copy(i, k).wait_send()
            weight_pass(i, k).wait_send()
        head_copy(k).wait_send()
        result_copy(k).wait_recv()
        result_copy(k).wait_send()
    out_ref[...] = resx[...].reshape(rows, LANES)


def shards(sizes, *args):
    x, ids, slots, counts, gain, wqk, wv, wo, fgain, wu, wd = args
    nz, nm, ns = sizes
    rows, width = x.shape
    owners = nz * ns
    cap = 2 * rows // owners
    groups = nz // 2
    per = 2 * ns
    grows = per * cap
    quarter = rows // nm
    vmem = pl.BlockSpec(memory_space=pltpu.VMEM)
    smem = pl.BlockSpec(memory_space=pltpu.SMEM)
    dma = pltpu.SemaphoreType.DMA
    return pl.pallas_call(
        functools.partial(block_kernel, sizes),
        out_shape=jax.ShapeDtypeStruct((rows, LANES), BF16),
        in_specs=[vmem, vmem, vmem, smem] + [vmem] * 7,
        out_specs=vmem,
        scratch_shapes=[
            pltpu.VMEM((rows, LANES), BF16),
            pltpu.VMEM((groups, per, cap, LANES), BF16),
            pltpu.VMEM((owners, 1, LANES), F32),
            pltpu.VMEM((groups, per, 1, LANES), F32),
            pltpu.VMEM((groups, per, cap, width), BF16),
            pltpu.VMEM((groups, grows, LANES), F32),
            pltpu.VMEM((rows, LANES), F32),
            pltpu.VMEM((WIN_DEV, WLEN, 3 * LANES), BF16),
            pltpu.VMEM((LANES, WIN_DEV * WLEN), BF16),
            pltpu.VMEM((groups, per, cap, LANES), BF16),
            pltpu.VMEM((groups, per, cap, LANES), BF16),
            pltpu.VMEM((nm, quarter, LANES), BF16),
            pltpu.VMEM((nm, quarter, LANES), BF16),
            pltpu.VMEM((nm, quarter, LANES), BF16),
            pltpu.VMEM((nm, quarter, LANES), BF16),
            pltpu.VMEM((nm,) + wo.shape, BF16),
            pltpu.VMEM((nm,) + wu.shape, BF16),
            pltpu.VMEM((nm,) + wd.shape, BF16),
            dma((groups,)),
            dma((groups,)),
            dma((groups,)),
            dma((groups,)),
            dma((groups, nm - 1)),
            dma((groups, nm - 1)),
            dma((groups,)),
            dma((groups,)),
            dma((3, nm - 1)),
            dma((3, nm - 1)),
            dma((3, nm - 1)),
            dma((3, nm - 1)),
            dma((nm - 1,)),
            dma((nm - 1,)),
            dma((nm - 1,)),
            dma((nm - 1,)),
        ],
        compiler_params=pltpu.CompilerParams(
            collective_id=0, has_side_effects=True, vmem_limit_bytes=60 * 1024 * 1024
        ),
        name="block",
    )(
        x,
        ids.reshape(1, rows),
        slots.reshape(1, rows),
        counts,
        gain.reshape(1, width),
        wqk,
        wv,
        wo,
        fgain.reshape(1, width),
        wu,
        wd,
    )


def solution(mesh):
    sizes = (mesh.shape["space"], mesh.shape["mp"], mesh.shape["sub"])
    return jax.shard_map(
        functools.partial(shards, sizes),
        mesh=mesh,
        in_specs=(
            P(("groups", "space", "sub"), None),
            P(("groups", "space", "sub")),
            P(("groups", "space", "sub")),
            P("groups"),
            P(),
            P(None, None, "mp"),
            P(None, "mp"),
            P("mp", None),
            P(),
            P(None, "mp"),
            P("mp", None),
        ),
        out_specs=P(("groups", "space", "sub"), "mp"),
        check_vma=False,
    )
```

time: 381 us -> 162 us (0.43)
  waiting for transfers between devices: 205 us -> 0 us
  Pallas kernels: 0 us -> 158 us
  local copies, waits for them, and re-layouts: 79.4 us -> 4.35 us
  starting transfers between devices: 43.8 us -> 0 us
  other arithmetic: 18 us -> 0 us
  matrix products: 14.5 us -> 0 us
  between operations: 13.8 us -> 0.01 us
  blocking collectives: 4.38 us -> 0 us
    all_to_all x4 -> x0, waiting for transfers between devices: 169 us -> none  [the longest x2 110 us: joined_exchange(): lax.all_to_all(pieces, axis, split_axis=0, concat_axis=0, tiled=True)]
    pallas_call x0 -> x1, Pallas kernels: none -> 158 us  [shards(): pl.pallas_call(functools.partial(block_kernel, sizes), out_shape=jax.Shap...]
    all_to_all x4 -> x0, starting transfers between devices: 43.5 us -> none  [the longest x2 35.7 us: joined_exchange(): lax.all_to_all(pieces, axis, split_axis=0, concat_axis=0, tiled=True)]
    all_gather x1 -> x0, waiting for transfers between devices: 36.2 us -> none  [rows_first(): whole = lax.all_gather(both, axis, axis=0, tiled=True)]
    scatter x3 -> x0, local copies, waits for them, and re-layouts: 31.8 us -> none  [the longest x1 16.2 us: shards(): padded = jnp.zeros((WIN_DEV * WLEN, row_width), jnp.bfloat16).at[arrived_...]
    reshape x5 -> x2, local copies, waits for them, and re-layouts: 19.5 us -> 2.58 us  [the longest x1 1.29 us: shards(): ids.reshape(1, rows)]
    gather x2 -> x0, local copies, waits for them, and re-layouts: 14.6 us -> none  [the longest x1 11.4 us: shards(): jnp.take(mixture, arrived_spots, axis=0, mode='clip')]
    dot_general x7 -> x0, matrix products: 14.5 us -> none  [the longest x1 5.36 us: feed_forward(): return jnp.dot(hidden, down_proj, preferred_element_type=jnp.float32)]
  transfers between devices with their start and end apart: 5 -> 0, of which waited for: 4 -> 0; matrix products, arithmetic and copies ran while one was open for 4% -> 0% of each run, Pallas kernels for 0% -> 0%
where the time goes in v1:
time: 162 us
  Pallas kernels  158 us (98%)
  local copies, waits for them, and re-layouts  4.35 us (3%)
    pallas_call x1, Pallas kernels, shards(): pl.pallas_call(functools.partial(block_kernel, sizes), out_shape=jax.Shap...  158 us

profile of v1, /device:TPU:168, one launch (start us, length us, event | category | flops | bytes accessed | tf_op | source)
XLA Modules:
  0.0 162.0 jit_solution(4692009939900144685)
XLA Ops:
  0.0 1.3 reshape.12.ids_ref
  1.3 1.3 reshape.13.slots_ref
  2.6 157.7 %block.1 = bf16[1536,128]{1,0:T(8,128)(2,1)} custom-call(bf16[1536,512]{1,0:T(8,128)(2,1)} %x_ref.1, s32[1,1536]{1,0:T(1,128)} %reshape.12.ids_ref, s32[1,1536]{1,0:T(1,128)} %reshape.13.slots_ref, s32[512]{0:T(512)} %counts_ref.1, f32[1,512]{1,0:T(1,128)} %bitcast.2, bf16[2,512,128]{2,1,0:T(8,128)(2,1)} %wqk_ref.1, bf16[512,128]{1,0:T(8,128)(2,1)} %wv_ref.1, ...), custom_call_target="tpu_custom_call" | custom-call | tf_op jit(solution)/shard_map/block/pallas_call | solution.py:484
  160.2 1.8 %copy.13 = bf16[1536,128]{1,0:T(8,128)(2,1)} copy(bf16[1536,128]{1,0:T(8,128)(2,1)} %block.1) | data formatting | bytes 786432

commit v2 on v1

--- a/solution.py
+++ b/solution.py
@@ -8,6 +8,8 @@
 from jax.sharding import PartitionSpec as P
 
 HDIM = 64
+CUTS = (2, 4, 6, 7)
+FFN_CUTS = (2, 4, 6, 7)
 WLEN = 256
 WIN_DEV = 16
 LANES = 128
@@ -30,6 +32,10 @@
 
 def pick(mask):
     return jnp.where(mask, 1.0, 0.0).astype(BF16)
+
+
+def pick16(mask):
+    return jnp.where(mask, jnp.ones((), BF16), jnp.zeros((), BF16))
 
 
 def block_kernel(
@@ -57,10 +63,12 @@
     mixt,
     ans,
     ret,
-    att,
-    attx,
+    xr,
+    hx,
     res,
-    resx,
+    rx,
+    f_send,
+    f_recv,
     wo_all,
     wu_all,
     wd_all,
@@ -74,6 +82,8 @@
     b_recv,
     w_send,
     w_recv,
+    v_send,
+    v_recv,
     d_send,
     d_recv,
     a_send,
@@ -88,7 +98,6 @@
     groups = nz // 2
     per = 2 * ns
     grows = per * cap
-    quarter = rows // nm
     z = lax.axis_index("space")
     m = lax.axis_index("mp")
     s = lax.axis_index("sub")
@@ -125,7 +134,11 @@
             device_id_type=MESH,
         )
 
-    order = [0] + list(range(groups - 1, 0, -1))
+    order = []
+    for g in range(1, groups // 2):
+        order += [g, groups - g]
+    order += [groups // 2, 0]
+    uses = sorted(order, key=lambda g: (groups if g == 0 else g) + 0.5 * order.index(g))
     others = [lax.rem(m + k, nm) for k in range(1, nm)]
 
     barrier = pltpu.get_barrier_semaphore()
@@ -220,6 +233,20 @@
                 sub=ts,
             ).start()
 
+    mine_iota = lax.broadcasted_iota(jnp.int32, (cap, 1), 0)
+
+    def mine_of(g):
+        near, far = (0, nz // 2) if g == 0 else (g, nz - g)
+        tz = lax.rem(z + jnp.where(m < ns, near, far), nz)
+        ts = lax.rem(s + lax.rem(m, ns), ns)
+        return mine_iota + (tz * ns + ts) * cap
+
+    def residual(part):
+        at = jnp.concatenate([mine_of(g) for g in part], axis=0)
+        got = dot(pick(at == send), x_ref[...]).astype(BF16)
+        for n, g in enumerate(part):
+            xr[g] = got[n * cap : (n + 1) * cap]
+
     arr[0, 0, :, mcols] = packed[0, 0]
     spot_in[0, 0] = spot_out[me]
     wo_all[m] = wo_ref[...]
@@ -261,18 +288,19 @@
             mp=others[0],
         ).wait_recv()
 
-    def share(g, k):
-        return remote(
-            arr.at[g, :, :, mcols],
-            arr.at[g, :, :, mcols],
-            x_send.at[g, k],
-            x_recv.at[g, k],
-            mp=others[k],
-        )
-
-    def shared_wait(g):
-        for k in range(nm - 1):
-            share(g, k).wait_recv()
+    sides = (lax.rem(m + 1, nm), lax.rem(m + nm - 1, nm))
+
+    def cols(who):
+        return pl.ds(pl.multiple_of(who * LANES, LANES), LANES)
+
+    def share(g, side):
+        ref = arr.at[g, :, :, mcols]
+        return remote(ref, ref, x_send.at[g, side], x_recv.at[g, side], mp=sides[side])
+
+    def share_on(g, side):
+        half = pl.ds(side * (per // 2), per // 2)
+        ref = arr.at[g, half, :, cols(sides[1 - side])]
+        return remote(ref, ref, f_send.at[g, side], f_recv.at[g, side], mp=sides[side])
 
     def regroup(pair, fresh):
         parts = []
@@ -283,82 +311,128 @@
                 spot_col[g, i * LANES : (i + 1) * LANES, :] = jnp.transpose(
                     jnp.broadcast_to(t, (LANES, LANES))
                 )
-        row = jnp.concatenate(parts, axis=1).astype(jnp.int32)
+        row = jnp.concatenate(parts, axis=1).astype(jnp.int32) - 1
+        row_win = row // WLEN
+        row_slot = (row - row_win * WLEN).astype(F32)
         held = jnp.concatenate([arr[g].reshape(grows, width) for g in pair], axis=0)
         proj = dot(held, wqkv).astype(BF16)
-        slot_iota = lax.broadcasted_iota(jnp.int32, (WLEN, row.shape[1]), 0) + 1
-
-        def one_window(w, carry):
-            got = dot(pick(slot_iota == row - w * WLEN), proj).astype(BF16)
+        slot_iota = lax.broadcasted_iota(jnp.int32, (WLEN, row.shape[1]), 0).astype(F32).astype(BF16)
+        few = 4
+
+        def some_windows(i, carry):
+            sels = []
+            for n in range(few):
+                key = jnp.where(row_win == i * few + n, row_slot, -1.0).astype(BF16)
+                sels.append(pick16(slot_iota == key))
+            got = dot(jnp.concatenate(sels, axis=0), proj).astype(BF16)
+            at = pl.ds(pl.multiple_of(i * (few * WLEN), few * WLEN), few * WLEN)
             if fresh:
-                acc[w] = got
+                acc[at, :] = got
             else:
-                acc[w] = acc[w] + got
+                acc[at, :] = acc[at, :] + got
             return carry
 
-        lax.fori_loop(0, WIN_DEV, one_window, 0)
-
-    pairs = [order[i : i + 2] for i in range(0, groups, 2)]
-    for i, pair in enumerate(pairs):
-        for g in pair:
-            gather_wait(g)
-            for k in range(nm - 1):
-                share(g, k).start()
-        if i > 0:
-            for g in pairs[i - 1]:
-                shared_wait(g)
-            regroup(pairs[i - 1], i == 1)
-
-    def weight_parts(ref, all_ref, who):
+        lax.fori_loop(0, WIN_DEV // few, some_windows, 0)
+
+    sets = [uses[a:b] for a, b in zip((0,) + CUTS, CUTS + (groups,))]
+
+    def stage(i):
+        if 0 <= i < groups:
+            gather_wait(uses[i])
+            for side in range(2):
+                share(uses[i], side).start()
+
+    def stage_on(i):
+        if 0 <= i < groups:
+            for side in range(2):
+                share(uses[i], side).wait_recv()
+                share_on(uses[i], side).start()
+
+    def stage_use(i):
+        for n, part in enumerate(sets):
+            if 0 <= i < groups and part[-1] == uses[i]:
+                for g in part:
+                    for side in range(2):
+                        share_on(g, side).wait_recv()
+                regroup(part, n == 0)
+
+    for i in range(groups):
+        stage(i)
+        stage_on(i - 1)
+        stage_use(i - 2)
+        if i in (2, 4):
+            residual(uses[:groups // 2] if i == 2 else uses[groups // 2:])
+    stage_on(groups - 1)
+
+    kept = ((wu_ref, wu_all), (wd_ref, wd_all), (wo_ref, wo_all))
+
+    def weight_copy(i, side):
+        ref, all_ref = kept[i]
         half = ref.shape[0] // ns
         at = pl.ds(pl.multiple_of(s * half, half), half)
-        return ref.at[at], all_ref.at[who, at]
-
-    def weight_copy(i, k):
-        ref, all_ref = ((wu_ref, wu_all), (wd_ref, wd_all), (wo_ref, wo_all))[i]
-        src, dst = weight_parts(ref, all_ref, m)
-        return remote(src, dst, w_send.at[i, k], w_recv.at[i, k], mp=others[k])
+        return remote(
+            ref.at[at], all_ref.at[m, at], w_send.at[i, side], w_recv.at[i, side], mp=sides[side]
+        )
+
+    def weight_on(i, side):
+        ref, all_ref = kept[i]
+        half = ref.shape[0] // ns
+        low = half // 2
+        at = pl.ds(pl.multiple_of(s * half + side * low, low), low)
+        part = all_ref.at[sides[1 - side], at]
+        return remote(part, part, v_send.at[i, side], v_recv.at[i, side], mp=sides[side])
 
     def weight_pass(i, k):
-        ref, all_ref = ((wu_ref, wu_all), (wd_ref, wd_all), (wo_ref, wo_all))[i]
-        src, dst = weight_parts(ref, all_ref, lax.rem(m + nm - 1 - k, nm))
-        return remote(dst, dst, d_send.at[i, k], d_recv.at[i, k], sub=lax.rem(s + 1, ns))
+        ref, all_ref = kept[i]
+        half = ref.shape[0] // ns
+        at = pl.ds(pl.multiple_of(s * half, half), half)
+        part = all_ref.at[others[k], at]
+        return remote(part, part, d_send.at[i, k], d_recv.at[i, k], sub=lax.rem(s + 1, ns))
+
+    def weights_on(side):
+        for i in range(3):
+            weight_copy(i, side).wait_recv()
+            weight_on(i, side).start()
 
     for i in range(3):
-        for k in range(nm - 1):
-            weight_copy(i, k).start()
-
-    for g in pairs[-1]:
-        shared_wait(g)
-    regroup(pairs[-1], False)
-
-    key_iota = lax.broadcasted_iota(jnp.int32, (WLEN, WLEN), 0)
-    head_of = lax.broadcasted_iota(jnp.int32, (1, LANES), 1) // HDIM
+        for side in range(2):
+            weight_copy(i, side).start()
+
+    stage_use(groups - 2)
+    stage_use(groups - 1)
+
+    key_iota = lax.broadcasted_iota(jnp.int32, (WLEN, LANES), 0)
+    heads_here = LANES // HDIM
+    head_of = lane // HDIM
+    own = [jnp.where(head_of == h, 1.0, 0.0).astype(BF16) for h in range(heads_here)]
+    extra = [jnp.where(lane == (heads_here - 1 - h) * HDIM, 1.0, 0.0) for h in range(heads_here)]
+    ones = jnp.ones((16, WLEN), BF16)
 
     def attend(w, carry):
-        here = acc[w]
-        q = here[:, :LANES]
+        at = pl.ds(pl.multiple_of(w * WLEN, WLEN), WLEN)
+        here = acc[at, :]
+        q = here[:, :LANES] * jnp.asarray(HDIM**-0.5, BF16)
         k = here[:, LANES : 2 * LANES]
         v = here[:, 2 * LANES :]
-        live = key_iota < counts_ref[me * WIN_DEV + w]
+        dead = jnp.where(key_iota < counts_ref[me * WIN_DEV + w], 0.0, -1e30)
         parts = []
         vt = jnp.transpose(v.astype(F32)).astype(BF16)
-        for h in range(LANES // HDIM):
-            qh = jnp.where(head_of == h, q.astype(F32) * HDIM**-0.5, 0.0).astype(BF16)
-            sc = jnp.where(live, dot_nt(k, qh), -1e30)
-            weights = jnp.exp(sc - jnp.max(sc, axis=0, keepdims=True))
-            total = jnp.sum(weights, axis=0, keepdims=True)
-            mix = dot(vt[h * HDIM : (h + 1) * HDIM], weights.astype(BF16))
-            parts.append(mix / total)
-        at = pl.ds(pl.multiple_of(w * WLEN, WLEN), WLEN)
+        for h in range(heads_here):
+            qh = q * own[h] + extra[h].astype(BF16)
+            kh = k * own[h] + (dead * extra[h]).astype(BF16)
+            sc = dot_nt(kh, qh)
+            weights = jnp.exp(sc - jnp.max(sc, axis=0, keepdims=True)).astype(BF16)
+            both = jnp.concatenate([vt[h * HDIM : (h + 1) * HDIM], ones], axis=0)
+            mix = dot(both, weights)
+            parts.append(mix[:HDIM] / mix[HDIM : HDIM + 1])
         mixt[:, at] = jnp.concatenate(parts, axis=0).astype(BF16)
         return carry
 
-    lax.fori_loop(0, WIN_DEV, attend, 0)
+    lax.fori_loop(0, WIN_DEV, attend, 0, unroll=2)
 
     span = 4 * WLEN
     span_iota = lax.broadcasted_iota(jnp.int32, (1, span), 1)
-    for g in order:
+    for n, g in enumerate(order):
         col = spot_col[g].astype(jnp.int32)
         wide = jnp.concatenate([col] * (span // LANES), axis=1)
 
@@ -375,72 +449,95 @@
             remote(
                 ans.at[g, j], ret.at[g, j], b_send.at[g], b_recv.at[g], space=tz, sub=ts
             ).start()
+        if n == 0:
+            for side in range(2):
+                weights_on(side)
     ret[0, 0] = ans[0, 0]
 
     for i in range(3):
+        for side in range(2):
+            weight_on(i, side).wait_recv()
         for k in range(nm - 1):
-            weight_copy(i, k).wait_recv()
             weight_pass(i, k).start()
+
+    def onward(g, k):
+        return remote(
+            ret.at[g, others[k]], hx.at[g, m], a_send.at[g, k], a_recv.at[g, k], mp=others[k]
+        )
+
+    def result_copy(g, k):
+        return remote(
+            res.at[g, others[k]], rx.at[g, m], r_send.at[g, k], r_recv.at[g, k], mp=others[k]
+        )
+
+    def come_back(i):
+        g = uses[i]
+        at = pl.ds(first(g), per - first(g))
+        remote(
+            ans.at[g, at], ret.at[g, at], b_send.at[g], b_recv.at[g], mp=others[0]
+        ).wait_recv()
+        for k in range(nm - 1):
+            onward(g, k).start()
+        hx[g, m] = ret[g, m]
+
+    def feed_forward(part):
+        for g in part:
+            for k in range(nm - 1):
+                onward(g, k).wait_recv()
+        heads = jnp.concatenate(
+            [jnp.concatenate([hx[g, k] for k in range(nm)], axis=1) for g in part], axis=0
+        )
+        stream = jnp.concatenate([xr[g] for g in part], axis=0).astype(F32)
+        after = stream + dot(heads, wo_all[...].reshape(width, width))
+        mean = jnp.sum(after, axis=1, keepdims=True) * (1.0 / width)
+        cen = after - mean
+        var = jnp.sum(cen * cen, axis=1, keepdims=True) * (1.0 / width)
+        normed = (cen * lax.rsqrt(var + 1e-05) * fgain_ref[...]).astype(BF16)
+        total = after
+        for c in range(nm):
+            up = dot(normed, wu_all[c])
+            inner = 0.7978845608028654 * (up + 0.044715 * (up * up * up))
+            hidden = (0.5 * up * (1.0 + jnp.tanh(inner))).astype(BF16)
+            total = total + dot(hidden, wd_all[c])
+        total = total.astype(BF16)
+        for n, g in enumerate(part):
+            for k in range(nm):
+                res[g, k] = total[n * cap : (n + 1) * cap, k * LANES : (k + 1) * LANES]
+            for k in range(nm - 1):
+                result_copy(g, k).start()
+            rx[g, m] = res[g, m]
 
     wide_send = send_col[...].astype(jnp.int32)
     wide_send = jnp.concatenate([wide_send] * (grows // LANES), axis=1)
-    for n, g in enumerate(order):
-        lo = first(g)
-        remote(
-            ans.at[g, pl.ds(lo, per - lo)],
-            ret.at[g, pl.ds(lo, per - lo)],
-            b_send.at[g],
-            b_recv.at[g],
-            mp=others[0],
-        ).wait_recv()
+
+    def finish(g, fresh):
+        for k in range(nm - 1):
+            result_copy(g, k).wait_recv()
         got = dot(
-            pick(wide_send == places(g, lane_in)), ret[g].reshape(grows, LANES)
+            pick(wide_send == places(g, lane_in)), rx[g].reshape(grows, LANES)
         ).astype(BF16)
-        got = got.reshape(nm, quarter, LANES)
-        if n == 0:
-            att[...] = got
+        if fresh:
+            out_ref[...] = got
         else:
-            att[...] = att[...] + got
-
-    def head_copy(k):
-        return remote(
-            att.at[others[k]], attx.at[m], a_send.at[k], a_recv.at[k], mp=others[k]
-        )
-
-    for k in range(nm - 1):
-        head_copy(k).start()
-    attx[m] = att[m]
-    for i in range(3):
-        for k in range(nm - 1):
-            weight_pass(i, k).wait_recv()
-    for k in range(nm - 1):
-        head_copy(k).wait_recv()
-
-    heads = jnp.concatenate([attx[k] for k in range(nm)], axis=1)
-    mine = pl.ds(pl.multiple_of(m * quarter, quarter), quarter)
-    after = x_ref[mine, :].astype(F32) + dot(heads, wo_all[...].reshape(width, width))
-    mean = jnp.sum(after, axis=1, keepdims=True) * (1.0 / width)
-    cen = after - mean
-    var = jnp.sum(cen * cen, axis=1, keepdims=True) * (1.0 / width)
-    normed = (cen * lax.rsqrt(var + 1e-05) * fgain_ref[...]).astype(BF16)
-    total = after
-    for c in range(nm):
-        up = dot(normed, wu_all[c])
-        inner = 0.7978845608028654 * (up + 0.044715 * (up * up * up))
-        hidden = (0.5 * up * (1.0 + jnp.tanh(inner))).astype(BF16)
-        total = total + dot(hidden, wd_all[c])
-    total = total.astype(BF16)
-    for k in range(nm):
-        res[k] = total[:, k * LANES : (k + 1) * LANES]
-
-    def result_copy(k):
-        return remote(
-            res.at[others[k]], resx.at[m], r_send.at[k], r_recv.at[k], mp=others[k]
-        )
-
-    for k in range(nm - 1):
-        result_copy(k).start()
-    resx[m] = res[m]
+            out_ref[...] = out_ref[...] + got
+
+    ffn_sets = [uses[a:b] for a, b in zip((0,) + FFN_CUTS, FFN_CUTS + (groups,))]
+    ready = []
+    for i in range(groups + 1):
+        if i < groups:
+            come_back(i)
+        for part in ffn_sets:
+            if i > 0 and part[-1] == uses[i - 1]:
+                if i == 2:
+                    for a in range(3):
+                        for k in range(nm - 1):
+                            weight_pass(a, k).wait_recv()
+                feed_forward(part)
+                for g in ready:
+                    finish(g, g == uses[0])
+                ready = part
+    for g in ready:
+        finish(g, False)
 
     for g in range(groups):
         lo = first(g)
@@ -456,16 +553,18 @@
             packed.at[g, at], arr.at[g, at, :, mcols], z_send.at[g], z_recv.at[g], mp=others[0]
         ).wait_send()
         remote(ans.at[g, at], ret.at[g, at], b_send.at[g], b_recv.at[g], mp=others[0]).wait_send()
+        for side in range(2):
+            share(g, side).wait_send()
+            share_on(g, side).wait_send()
         for k in range(nm - 1):
-            share(g, k).wait_send()
-    for k in range(nm - 1):
-        for i in range(3):
-            weight_copy(i, k).wait_send()
+            onward(g, k).wait_send()
+            result_copy(g, k).wait_send()
+    for i in range(3):
+        for side in range(2):
+            weight_copy(i, side).wait_send()
+            weight_on(i, side).wait_send()
+        for k in range(nm - 1):
             weight_pass(i, k).wait_send()
-        head_copy(k).wait_send()
-        result_copy(k).wait_recv()
-        result_copy(k).wait_send()
-    out_ref[...] = resx[...].reshape(rows, LANES)
 
 
 def shards(sizes, *args):
@@ -477,7 +576,6 @@
     groups = nz // 2
     per = 2 * ns
     grows = per * cap
-    quarter = rows // nm
     vmem = pl.BlockSpec(memory_space=pltpu.VMEM)
     smem = pl.BlockSpec(memory_space=pltpu.SMEM)
     dma = pltpu.SemaphoreType.DMA
@@ -494,14 +592,16 @@
             pltpu.VMEM((groups, per, cap, width), BF16),
             pltpu.VMEM((groups, grows, LANES), F32),
             pltpu.VMEM((rows, LANES), F32),
-            pltpu.VMEM((WIN_DEV, WLEN, 3 * LANES), BF16),
+            pltpu.VMEM((WIN_DEV * WLEN, 3 * LANES), BF16),
             pltpu.VMEM((LANES, WIN_DEV * WLEN), BF16),
             pltpu.VMEM((groups, per, cap, LANES), BF16),
             pltpu.VMEM((groups, per, cap, LANES), BF16),
-            pltpu.VMEM((nm, quarter, LANES), BF16),
-            pltpu.VMEM((nm, quarter, LANES), BF16),
-            pltpu.VMEM((nm, quarter, LANES), BF16),
-            pltpu.VMEM((nm, quarter, LANES), BF16),
+            pltpu.VMEM((groups, cap, width), BF16),
+            pltpu.VMEM((groups, nm, cap, LANES), BF16),
+            pltpu.VMEM((groups, nm, cap, LANES), BF16),
+            pltpu.VMEM((groups, nm, cap, LANES), BF16),
+            dma((groups, 2)),
+            dma((groups, 2)),
             pltpu.VMEM((nm,) + wo.shape, BF16),
             pltpu.VMEM((nm,) + wu.shape, BF16),
             pltpu.VMEM((nm,) + wd.shape, BF16),
@@ -509,18 +609,20 @@
             dma((groups,)),
             dma((groups,)),
             dma((groups,)),
+            dma((groups, 2)),
+            dma((groups, 2)),
+            dma((groups,)),
+            dma((groups,)),
+            dma((3, 2)),
+            dma((3, 2)),
+            dma((3, 2)),
+            dma((3, 2)),
+            dma((3, nm - 1)),
+            dma((3, nm - 1)),
             dma((groups, nm - 1)),
             dma((groups, nm - 1)),
-            dma((groups,)),
-            dma((groups,)),
-            dma((3, nm - 1)),
-            dma((3, nm - 1)),
-            dma((3, nm - 1)),
-            dma((3, nm - 1)),
-            dma((nm - 1,)),
-            dma((nm - 1,)),
-            dma((nm - 1,)),
-            dma((nm - 1,)),
+            dma((groups, nm - 1)),
+            dma((groups, nm - 1)),
         ],
         compiler_params=pltpu.CompilerParams(
             collective_id=0, has_side_effects=True, vmem_limit_bytes=60 * 1024 * 1024

time: 162 us -> 176 us (1.086)
  Pallas kernels: 158 us -> 171 us
    pallas_call x1, Pallas kernels: 158 us -> 171 us  [shards(): pl.pallas_call(functools.partial(block_kernel, sizes), out_shape=jax.Shap...]
where the time goes in v2:
time: 176 us; the launch traced here: 175 us
  Pallas kernels  171 us (97%)
  local copies, waits for them, and re-layouts  4.35 us (2%)
    pallas_call x1, Pallas kernels, shards(): pl.pallas_call(functools.partial(block_kernel, sizes), out_shape=jax.Shap...  171 us

profile of v2, /device:TPU:168, one launch (start us, length us, event | category | flops | bytes accessed | tf_op | source)
XLA Modules:
  0.0 175.5 jit_solution(2766424278472194209)
XLA Ops:
  0.0 1.3 reshape.12.ids_ref
  1.3 1.3 reshape.13.slots_ref
  2.6 171.1 %block.1 = bf16[1536,128]{1,0:T(8,128)(2,1)} custom-call(bf16[1536,512]{1,0:T(8,128)(2,1)} %x_ref.1, s32[1,1536]{1,0:T(1,128)} %reshape.12.ids_ref, s32[1,1536]{1,0:T(1,128)} %reshape.13.slots_ref, s32[512]{0:T(512)} %counts_ref.1, f32[1,512]{1,0:T(1,128)} %bitcast.2, bf16[2,512,128]{2,1,0:T(8,128)(2,1)} %wqk_ref.1, bf16[512,128]{1,0:T(8,128)(2,1)} %wv_ref.1, ...), custom_call_target="tpu_custom_call" | custom-call | tf_op jit(solution)/shard_map/block/pallas_call | solution.py:582
  173.7 1.8 %copy.13 = bf16[1536,128]{1,0:T(8,128)(2,1)} copy(bf16[1536,128]{1,0:T(8,128)(2,1)} %block.1) | data formatting | bytes 786432

commit v3 on v2

--- a/solution.py
+++ b/solution.py
@@ -8,7 +8,9 @@
 from jax.sharding import PartitionSpec as P
 
 HDIM = 64
-CUTS = (2, 4, 6, 7)
+CUTS = (1, 2, 3, 4, 5, 6, 7)
+AHEAD = 8
+BACK = 8
 FFN_CUTS = (2, 4, 6, 7)
 WLEN = 256
 WIN_DEV = 16
@@ -63,6 +65,8 @@
     mixt,
     ans,
     ret,
+    sc_even,
+    sc_odd,
     xr,
     hx,
     res,
@@ -134,11 +138,8 @@
             device_id_type=MESH,
         )
 
-    order = []
-    for g in range(1, groups // 2):
-        order += [g, groups - g]
-    order += [groups // 2, 0]
-    uses = sorted(order, key=lambda g: (groups if g == 0 else g) + 0.5 * order.index(g))
+    order = list(range(1, groups)) + [0]
+    uses = order
     others = [lax.rem(m + k, nm) for k in range(1, nm)]
 
     barrier = pltpu.get_barrier_semaphore()
@@ -163,7 +164,7 @@
 
     lax.fori_loop(0, rows // 256, norm_rows, 0)
 
-    ids = ids_ref[...]
+    ids = ids_ref[...].reshape(1, rows)
     dest = ids // WIN_DEV
     win = ids - dest * WIN_DEV
     owner_iota = lax.broadcasted_iota(jnp.int32, (owners, rows), 0)
@@ -186,7 +187,7 @@
     send = dest * cap + rank
     rank_hit = pick(lax.broadcasted_iota(jnp.int32, (LANES, rows), 0) == rank)
     slot_at = dot_nt(
-        jnp.where(hit, (slots_ref[...] + 1).astype(F32), 0.0).astype(BF16), rank_hit
+        jnp.where(hit, (slots_ref[...].reshape(1, rows) + 1).astype(F32), 0.0).astype(BF16), rank_hit
     )
     win_at = dot_nt(jnp.where(hit, win.astype(F32), 0.0).astype(BF16), rank_hit)
     spots = slot_at + win_at * float(WLEN)
@@ -208,7 +209,6 @@
                 total = jnp.where(inner >= j * cap, inner + low, total)
         return total
 
-    xn_all = xn[...]
     for g in order:
         for j in range(first(g), per):
             tz, ts = forward(g, j)
@@ -220,18 +220,29 @@
                 space=tz,
                 sub=ts,
             ).start()
+
+    def pack(g):
         sel = pick(places(g, row_in) == send)
-        packed[g] = dot(sel, xn_all).astype(BF16).reshape(per, cap, LANES)
-        for j in range(first(g), per):
-            tz, ts = forward(g, j)
-            remote(
-                packed.at[g, j],
-                arr.at[g, j, :, mcols],
-                z_send.at[g],
-                z_recv.at[g],
-                space=tz,
-                sub=ts,
-            ).start()
+        packed[g] = dot(sel, xn[...]).astype(BF16).reshape(per, cap, LANES)
+
+    def post(i):
+        if i < groups:
+            g = order[i]
+            for j in range(first(g), per):
+                tz, ts = forward(g, j)
+                remote(
+                    packed.at[g, j],
+                    arr.at[g, j, :, mcols],
+                    z_send.at[g],
+                    z_recv.at[g],
+                    space=tz,
+                    sub=ts,
+                ).start()
+
+    for i in range(groups):
+        pack(order[i])
+        if i < AHEAD:
+            post(i)
 
     mine_iota = lax.broadcasted_iota(jnp.int32, (cap, 1), 0)
 
@@ -339,6 +350,7 @@
     def stage(i):
         if 0 <= i < groups:
             gather_wait(uses[i])
+            post(i + AHEAD)
             for side in range(2):
                 share(uses[i], side).start()
 
@@ -358,12 +370,10 @@
 
     for i in range(groups):
         stage(i)
-        stage_on(i - 1)
-        stage_use(i - 2)
+        stage_use(i - 1)
+        stage_on(i)
         if i in (2, 4):
             residual(uses[:groups // 2] if i == 2 else uses[groups // 2:])
-    stage_on(groups - 1)
-
     kept = ((wu_ref, wu_all), (wd_ref, wd_all), (wo_ref, wo_all))
 
     def weight_copy(i, side):
@@ -398,7 +408,6 @@
         for side in range(2):
             weight_copy(i, side).start()
 
-    stage_use(groups - 2)
     stage_use(groups - 1)
 
     key_iota = lax.broadcasted_iota(jnp.int32, (WLEN, LANES), 0)
@@ -408,30 +417,50 @@
     extra = [jnp.where(lane == (heads_here - 1 - h) * HDIM, 1.0, 0.0) for h in range(heads_here)]
     ones = jnp.ones((16, WLEN), BF16)
 
-    def attend(w, carry):
-        at = pl.ds(pl.multiple_of(w * WLEN, WLEN), WLEN)
-        here = acc[at, :]
+    def score(w, sc_ref):
+        here = acc[pl.ds(pl.multiple_of(w * WLEN, WLEN), WLEN), :]
         q = here[:, :LANES] * jnp.asarray(HDIM**-0.5, BF16)
         k = here[:, LANES : 2 * LANES]
-        v = here[:, 2 * LANES :]
         dead = jnp.where(key_iota < counts_ref[me * WIN_DEV + w], 0.0, -1e30)
-        parts = []
-        vt = jnp.transpose(v.astype(F32)).astype(BF16)
         for h in range(heads_here):
             qh = q * own[h] + extra[h].astype(BF16)
             kh = k * own[h] + (dead * extra[h]).astype(BF16)
-            sc = dot_nt(kh, qh)
+            sc_ref[h] = dot_nt(kh, qh)
+
+    def mix(w, sc_ref):
+        at = pl.ds(pl.multiple_of(w * WLEN, WLEN), WLEN)
+        vt = jnp.transpose(acc[at, 2 * LANES :].astype(F32)).astype(BF16)
+        parts = []
+        for h in range(heads_here):
+            sc = sc_ref[h]
             weights = jnp.exp(sc - jnp.max(sc, axis=0, keepdims=True)).astype(BF16)
             both = jnp.concatenate([vt[h * HDIM : (h + 1) * HDIM], ones], axis=0)
-            mix = dot(both, weights)
-            parts.append(mix[:HDIM] / mix[HDIM : HDIM + 1])
+            got = dot(both, weights)
+            parts.append(got[:HDIM] / got[HDIM : HDIM + 1])
         mixt[:, at] = jnp.concatenate(parts, axis=0).astype(BF16)
+
+    def attend(i, carry):
+        score(2 * i + 1, sc_odd)
+        mix(2 * i, sc_even)
+        score(jnp.minimum(2 * i + 2, WIN_DEV - 1), sc_even)
+        mix(2 * i + 1, sc_odd)
         return carry
 
-    lax.fori_loop(0, WIN_DEV, attend, 0, unroll=2)
+    score(0, sc_even)
+    lax.fori_loop(0, WIN_DEV // 2, attend, 0)
 
     span = 4 * WLEN
     span_iota = lax.broadcasted_iota(jnp.int32, (1, span), 1)
+
+    def answer(i):
+        if i < groups:
+            g = order[i]
+            for j in range(first(g), per):
+                tz, ts = backward(g, j)
+                remote(
+                    ans.at[g, j], ret.at[g, j], b_send.at[g], b_recv.at[g], space=tz, sub=ts
+                ).start()
+
     for n, g in enumerate(order):
         col = spot_col[g].astype(jnp.int32)
         wide = jnp.concatenate([col] * (span // LANES), axis=1)
@@ -444,11 +473,8 @@
             0, WIN_DEV * WLEN // span, gather, jnp.zeros((grows, LANES), F32)
         )
         ans[g] = total.astype(BF16).reshape(per, cap, LANES)
-        for j in range(first(g), per):
-            tz, ts = backward(g, j)
-            remote(
-                ans.at[g, j], ret.at[g, j], b_send.at[g], b_recv.at[g], space=tz, sub=ts
-            ).start()
+        if n < BACK:
+            answer(n)
         if n == 0:
             for side in range(2):
                 weights_on(side)
@@ -476,6 +502,7 @@
         remote(
             ans.at[g, at], ret.at[g, at], b_send.at[g], b_recv.at[g], mp=others[0]
         ).wait_recv()
+        answer(i + BACK)
         for k in range(nm - 1):
             onward(g, k).start()
         hx[g, m] = ret[g, m]
@@ -596,6 +623,8 @@
             pltpu.VMEM((LANES, WIN_DEV * WLEN), BF16),
             pltpu.VMEM((groups, per, cap, LANES), BF16),
             pltpu.VMEM((groups, per, cap, LANES), BF16),
+            pltpu.VMEM((LANES // HDIM, WLEN, WLEN), F32),
+            pltpu.VMEM((LANES // HDIM, WLEN, WLEN), F32),
             pltpu.VMEM((groups, cap, width), BF16),
             pltpu.VMEM((groups, nm, cap, LANES), BF16),
             pltpu.VMEM((groups, nm, cap, LANES), BF16),
@@ -630,8 +659,8 @@
         name="block",
     )(
         x,
-        ids.reshape(1, rows),
-        slots.reshape(1, rows),
+        ids,
+        slots,
         counts,
         gain.reshape(1, width),
         wqk,

time: 176 us -> 153 us (0.87)
  Pallas kernels: 171 us -> 151 us
  local copies, waits for them, and re-layouts: 4.35 us -> 1.77 us
    pallas_call x1, Pallas kernels: 171 us -> 151 us  [shards(): pl.pallas_call(functools.partial(block_kernel, sizes), out_shape=jax.Shap...]
    reshape x2 -> x0, local copies, waits for them, and re-layouts: 2.58 us -> none  [the longest x1 1.29 us: shards(): ids.reshape(1, rows)]
where the time goes in v3:
time: 153 us
  Pallas kernels  151 us (99%)
  local copies, waits for them, and re-layouts  1.77 us (1%)
    pallas_call x1, Pallas kernels, shards(): pl.pallas_call(functools.partial(block_kernel, sizes), out_shape=jax.Shap...  151 us

profile of v3, /device:TPU:168, one launch (start us, length us, event | category | flops | bytes accessed | tf_op | source)
XLA Modules:
  0.0 152.7 jit_solution(12279207840544876178)
XLA Ops:
  0.0 150.9 %block.1 = bf16[1536,128]{1,0:T(8,128)(2,1)} custom-call(bf16[1536,512]{1,0:T(8,128)(2,1)} %x_ref.1, s32[1536]{0:T(1024)} %ids_ref.1, s32[1536]{0:T(1024)} %slots_ref.1, s32[512]{0:T(512)} %counts_ref.1, f32[1,512]{1,0:T(1,128)} %bitcast.2, bf16[2,512,128]{2,1,0:T(8,128)(2,1)} %wqk_ref.1, bf16[512,128]{1,0:T(8,128)(2,1)} %wv_ref.1, bf16[128,512]{1,0:T(8,128)(2,1)} %wo_ref.1, ...), custom_call_target="tpu_custom_call" | custom-call | tf_op jit(solution)/shard_map/block/pallas_call | solution.py:609
  151.0 1.8 %copy.13 = bf16[1536,128]{1,0:T(8,128)(2,1)} copy(bf16[1536,128]{1,0:T(8,128)(2,1)} %block.1) | data formatting | bytes 786432

commit v4 on v3

--- a/solution.py
+++ b/solution.py
@@ -11,6 +11,7 @@
 CUTS = (1, 2, 3, 4, 5, 6, 7)
 AHEAD = 8
 BACK = 8
+LAG = 3
 FFN_CUTS = (2, 4, 6, 7)
 WLEN = 256
 WIN_DEV = 16
@@ -345,6 +346,46 @@
 
         lax.fori_loop(0, WIN_DEV // few, some_windows, 0)
 
+    kept = ((wu_ref, wu_all), (wd_ref, wd_all), (wo_ref, wo_all))
+
+    def weight_copy(i, side):
+        ref, all_ref = kept[i]
+        half = ref.shape[0] // ns
+        at = pl.ds(pl.multiple_of(s * half, half), half)
+        return remote(
+            ref.at[at], all_ref.at[m, at], w_send.at[i, side], w_recv.at[i, side], mp=sides[side]
+        )
+
+    def weight_on(i, side):
+        ref, all_ref = kept[i]
+        half = ref.shape[0] // ns
+        low = half // 2
+        at = pl.ds(pl.multiple_of(s * half + side * low, low), low)
+        part = all_ref.at[sides[1 - side], at]
+        return remote(part, part, v_send.at[i, side], v_recv.at[i, side], mp=sides[side])
+
+    def weight_pass(i, k):
+        ref, all_ref = kept[i]
+        half = ref.shape[0] // ns
+        at = pl.ds(pl.multiple_of(s * half, half), half)
+        part = all_ref.at[others[k], at]
+        return remote(part, part, d_send.at[i, k], d_recv.at[i, k], sub=lax.rem(s + 1, ns))
+
+    def weights_out(i):
+        for side in range(2):
+            weight_copy(i, side).start()
+
+    def weights_on(i):
+        for side in range(2):
+            weight_copy(i, side).wait_recv()
+            weight_on(i, side).start()
+
+    def weights_pass(i):
+        for side in range(2):
+            weight_on(i, side).wait_recv()
+        for k in range(nm - 1):
+            weight_pass(i, k).start()
+
     sets = [uses[a:b] for a, b in zip((0,) + CUTS, CUTS + (groups,))]
 
     def stage(i):
@@ -372,42 +413,15 @@
         stage(i)
         stage_use(i - 1)
         stage_on(i)
+        if i in (3, 4, 5):
+            weights_out(i - 3)
+        if i == 5:
+            weights_on(0)
+        if i == 6:
+            weights_on(1)
+            weights_on(2)
         if i in (2, 4):
             residual(uses[:groups // 2] if i == 2 else uses[groups // 2:])
-    kept = ((wu_ref, wu_all), (wd_ref, wd_all), (wo_ref, wo_all))
-
-    def weight_copy(i, side):
-        ref, all_ref = kept[i]
-        half = ref.shape[0] // ns
-        at = pl.ds(pl.multiple_of(s * half, half), half)
-        return remote(
-            ref.at[at], all_ref.at[m, at], w_send.at[i, side], w_recv.at[i, side], mp=sides[side]
-        )
-
-    def weight_on(i, side):
-        ref, all_ref = kept[i]
-        half = ref.shape[0] // ns
-        low = half // 2
-        at = pl.ds(pl.multiple_of(s * half + side * low, low), low)
-        part = all_ref.at[sides[1 - side], at]
-        return remote(part, part, v_send.at[i, side], v_recv.at[i, side], mp=sides[side])
-
-    def weight_pass(i, k):
-        ref, all_ref = kept[i]
-        half = ref.shape[0] // ns
-        at = pl.ds(pl.multiple_of(s * half, half), half)
-        part = all_ref.at[others[k], at]
-        return remote(part, part, d_send.at[i, k], d_recv.at[i, k], sub=lax.rem(s + 1, ns))
-
-    def weights_on(side):
-        for i in range(3):
-            weight_copy(i, side).wait_recv()
-            weight_on(i, side).start()
-
-    for i in range(3):
-        for side in range(2):
-            weight_copy(i, side).start()
-
     stage_use(groups - 1)
 
     key_iota = lax.broadcasted_iota(jnp.int32, (WLEN, LANES), 0)
@@ -461,31 +475,6 @@
                     ans.at[g, j], ret.at[g, j], b_send.at[g], b_recv.at[g], space=tz, sub=ts
                 ).start()
 
-    for n, g in enumerate(order):
-        col = spot_col[g].astype(jnp.int32)
-        wide = jnp.concatenate([col] * (span // LANES), axis=1)
-
-        def gather(c, total):
-            at = pl.ds(pl.multiple_of(c * span, span), span)
-            return total + dot_nt(pick(wide == span_iota + (c * span + 1)), mixt[:, at])
-
-        total = lax.fori_loop(
-            0, WIN_DEV * WLEN // span, gather, jnp.zeros((grows, LANES), F32)
-        )
-        ans[g] = total.astype(BF16).reshape(per, cap, LANES)
-        if n < BACK:
-            answer(n)
-        if n == 0:
-            for side in range(2):
-                weights_on(side)
-    ret[0, 0] = ans[0, 0]
-
-    for i in range(3):
-        for side in range(2):
-            weight_on(i, side).wait_recv()
-        for k in range(nm - 1):
-            weight_pass(i, k).start()
-
     def onward(g, k):
         return remote(
             ret.at[g, others[k]], hx.at[g, m], a_send.at[g, k], a_recv.at[g, k], mp=others[k]
@@ -506,6 +495,27 @@
         for k in range(nm - 1):
             onward(g, k).start()
         hx[g, m] = ret[g, m]
+
+    for n, g in enumerate(order):
+        col = spot_col[g].astype(jnp.int32)
+        wide = jnp.concatenate([col] * (span // LANES), axis=1)
+
+        def gather(c, total):
+            at = pl.ds(pl.multiple_of(c * span, span), span)
+            return total + dot_nt(pick(wide == span_iota + (c * span + 1)), mixt[:, at])
+
+        total = lax.fori_loop(
+            0, WIN_DEV * WLEN // span, gather, jnp.zeros((grows, LANES), F32)
+        )
+        ans[g] = total.astype(BF16).reshape(per, cap, LANES)
+        if g == 0:
+            ret[0, 0] = ans[0, 0]
+        if n < BACK:
+            answer(n)
+        if n < 3:
+            weights_pass(n)
+        if n >= LAG:
+            come_back(n - LAG)
 
     def feed_forward(part):
         for g in part:
@@ -551,7 +561,7 @@
     ffn_sets = [uses[a:b] for a, b in zip((0,) + FFN_CUTS, FFN_CUTS + (groups,))]
     ready = []
     for i in range(groups + 1):
-        if i < groups:
+        if groups - LAG <= i < groups:
             come_back(i)
         for part in ffn_sets:
             if i > 0 and part[-1] == uses[i - 1]:

time: 153 us -> 164 us (1.072)
  Pallas kernels: 151 us -> 161 us
    pallas_call x1, Pallas kernels: 151 us -> 161 us  [shards(): pl.pallas_call(functools.partial(block_kernel, sizes), out_shape=jax.Shap...]
where the time goes in v4:
time: 164 us; the launch traced here: 163 us
  Pallas kernels  161 us (98%)
  local copies, waits for them, and re-layouts  1.77 us (1%)
    pallas_call x1, Pallas kernels, shards(): pl.pallas_call(functools.partial(block_kernel, sizes), out_shape=jax.Shap...  161 us

profile of v4, /device:TPU:168, one launch (start us, length us, event | category | flops | bytes accessed | tf_op | source)
XLA Modules:
  0.0 163.3 jit_solution(16273347779438209633)
XLA Ops:
  0.0 161.5 %block.1 = bf16[1536,128]{1,0:T(8,128)(2,1)} custom-call(bf16[1536,512]{1,0:T(8,128)(2,1)} %x_ref.1, s32[1536]{0:T(1024)} %ids_ref.1, s32[1536]{0:T(1024)} %slots_ref.1, s32[512]{0:T(512)} %counts_ref.1, f32[1,512]{1,0:T(1,128)} %bitcast.2, bf16[2,512,128]{2,1,0:T(8,128)(2,1)} %wqk_ref.1, bf16[512,128]{1,0:T(8,128)(2,1)} %wv_ref.1, bf16[128,512]{1,0:T(8,128)(2,1)} %wo_ref.1, ...), custom_call_target="tpu_custom_call" | custom-call | tf_op jit(solution)/shard_map/block/pallas_call | solution.py:619
  161.5 1.8 %copy.13 = bf16[1536,128]{1,0:T(8,128)(2,1)} copy(bf16[1536,128]{1,0:T(8,128)(2,1)} %block.1) | data formatting | bytes 786432

commit v5 on v3

--- a/solution.py
+++ b/solution.py
@@ -475,16 +475,10 @@
         ans[g] = total.astype(BF16).reshape(per, cap, LANES)
         if n < BACK:
             answer(n)
-        if n == 0:
+        if n == groups // 2:
             for side in range(2):
                 weights_on(side)
     ret[0, 0] = ans[0, 0]
-
-    for i in range(3):
-        for side in range(2):
-            weight_on(i, side).wait_recv()
-        for k in range(nm - 1):
-            weight_pass(i, k).start()
 
     def onward(g, k):
         return remote(
@@ -553,6 +547,12 @@
     for i in range(groups + 1):
         if i < groups:
             come_back(i)
+        if i == 1:
+            for a in range(3):
+                for side in range(2):
+                    weight_on(a, side).wait_recv()
+                for k in range(nm - 1):
+                    weight_pass(a, k).start()
         for part in ffn_sets:
             if i > 0 and part[-1] == uses[i - 1]:
                 if i == 2:

time: 153 us -> 153 us (level)
  no operation moved by 1% of the time
where the time goes in v5:
time: 153 us
  Pallas kernels  151 us (99%)
  local copies, waits for them, and re-layouts  1.77 us (1%)
    pallas_call x1, Pallas kernels, shards(): pl.pallas_call(functools.partial(block_kernel, sizes), out_shape=jax.Shap...  151 us

profile of v5, /device:TPU:168, one launch (start us, length us, event | category | flops | bytes accessed | tf_op | source)
XLA Modules:
  0.0 152.9 jit_solution(2639085833031895381)
XLA Ops:
  0.0 151.1 %block.1 = bf16[1536,128]{1,0:T(8,128)(2,1)} custom-call(bf16[1536,512]{1,0:T(8,128)(2,1)} %x_ref.1, s32[1536]{0:T(1024)} %ids_ref.1, s32[1536]{0:T(1024)} %slots_ref.1, s32[512]{0:T(512)} %counts_ref.1, f32[1,512]{1,0:T(1,128)} %bitcast.2, bf16[2,512,128]{2,1,0:T(8,128)(2,1)} %wqk_ref.1, bf16[512,128]{1,0:T(8,128)(2,1)} %wv_ref.1, bf16[128,512]{1,0:T(8,128)(2,1)} %wo_ref.1, ...), custom_call_target="tpu_custom_call" | custom-call | tf_op jit(solution)/shard_map/block/pallas_call | solution.py:609
  151.1 1.8 %copy.13 = bf16[1536,128]{1,0:T(8,128)(2,1)} copy(bf16[1536,128]{1,0:T(8,128)(2,1)} %block.1) | data formatting | bytes 786432

commit v6 on v3

--- a/solution.py
+++ b/solution.py
@@ -450,7 +450,8 @@
     lax.fori_loop(0, WIN_DEV // 2, attend, 0)
 
     span = 4 * WLEN
-    span_iota = lax.broadcasted_iota(jnp.int32, (1, span), 1)
+    lane_iota = lax.broadcasted_iota(jnp.int32, (grows, LANES), 1)
+    lane_tiles = [(lane_iota + i).astype(F32).astype(BF16) for i in range(0, WLEN, LANES)]
 
     def answer(i):
         if i < groups:
@@ -462,12 +463,17 @@
                 ).start()
 
     for n, g in enumerate(order):
-        col = spot_col[g].astype(jnp.int32)
-        wide = jnp.concatenate([col] * (span // LANES), axis=1)
+        col = spot_col[g].astype(jnp.int32) - 1
+        col_win = col // WLEN
+        col_slot = (col - col_win * WLEN).astype(F32)
 
         def gather(c, total):
             at = pl.ds(pl.multiple_of(c * span, span), span)
-            return total + dot_nt(pick(wide == span_iota + (c * span + 1)), mixt[:, at])
+            tiles = []
+            for n in range(span // WLEN):
+                key = jnp.where(col_win == c * (span // WLEN) + n, col_slot, -1.0).astype(BF16)
+                tiles += [pick16(key == tile) for tile in lane_tiles]
+            return total + dot_nt(jnp.concatenate(tiles, axis=1), mixt[:, at])
 
         total = lax.fori_loop(
             0, WIN_DEV * WLEN // span, gather, jnp.zeros((grows, LANES), F32)

time: 153 us -> 154 us (level)
  no operation moved by 1% of the time
where the time goes in v6:
time: 154 us
  Pallas kernels  152 us (99%)
  local copies, waits for them, and re-layouts  1.77 us (1%)
    pallas_call x1, Pallas kernels, shards(): pl.pallas_call(functools.partial(block_kernel, sizes), out_shape=jax.Shap...  152 us

profile of v6, /device:TPU:168, one launch (start us, length us, event | category | flops | bytes accessed | tf_op | source)
XLA Modules:
  0.0 153.8 jit_solution(13107781271335509656)
XLA Ops:
  0.0 152.0 %block.1 = bf16[1536,128]{1,0:T(8,128)(2,1)} custom-call(bf16[1536,512]{1,0:T(8,128)(2,1)} %x_ref.1, s32[1536]{0:T(1024)} %ids_ref.1, s32[1536]{0:T(1024)} %slots_ref.1, s32[512]{0:T(512)} %counts_ref.1, f32[1,512]{1,0:T(1,128)} %bitcast.2, bf16[2,512,128]{2,1,0:T(8,128)(2,1)} %wqk_ref.1, bf16[512,128]{1,0:T(8,128)(2,1)} %wv_ref.1, bf16[128,512]{1,0:T(8,128)(2,1)} %wo_ref.1, ...), custom_call_target="tpu_custom_call" | custom-call | tf_op jit(solution)/shard_map/block/pallas_call | solution.py:615
  152.0 1.8 %copy.13 = bf16[1536,128]{1,0:T(8,128)(2,1)} copy(bf16[1536,128]{1,0:T(8,128)(2,1)} %block.1) | data formatting | bytes 786432
